TPU v7x, 32 devices: a whole 2x2x4 slice. The times are simulated.
32 devices in a mesh: row: 8 (over y, x, core), col: 4 (over z).
Axes of the slice: x: 2, y: 2, z: 4, core: 2. Of those that a mesh axis runs over, the one named last changes fastest.
Arguments:
- choi: float32 [4, 2048, 1024], P(None, 'row', 'col'), may hold values from -0.5 to 8, as said below
Outputs:
- factored: float32 [4, 2048, 1024], P(None, 'row', 'col')
Inputs may be any that keep to these rules, and one draw needn't show every extreme that they name: `choi`: the leading 1024 x 1024 block of the matrix is symmetric with a positive diagonal, and its leading 2 * 256 square is positive definite.
All inputs are finite; a program needn't handle non-finite values.
Results may differ from a plain program's by a relative error of at most 0.0001.
Values sent between devices are 32-bit elements; how exact they have to be, the bound alone decides.
A program may use at most 64 MiB of HBM per device.

v0:
```python
import jax
import jax.numpy as jnp
from jax import lax
from jax.sharding import PartitionSpec as P

PANELS = 2


def broadcast(value, axis, source):
    kept = jnp.where(lax.axis_index(axis) == source, value, 0).astype(value.dtype)
    return lax.psum(kept, axis)


def factor_tile(diagonal):
    tile_size = diagonal.shape[0]
    identity = jnp.eye(tile_size, dtype=jnp.float32)
    factor = jnp.linalg.cholesky(diagonal)
    inverse = jax.scipy.linalg.solve_triangular(factor, identity, lower=True)
    return (factor, inverse)


def panel_from(blocks, factor, inverse, tile_index, step):
    beneath = jnp.einsum("sij,kj->sik", blocks, inverse, precision=lax.Precision.HIGHEST)
    place = tile_index[:, None, None]
    return jnp.where(place > step, beneath, jnp.where(place == step, factor[None], 0.0))


def body(choi):
    slot_count = choi.shape[0]
    row_count = lax.axis_size("row")
    my_row = lax.axis_index("row")
    my_col = lax.axis_index("col")
    tile_index = jnp.arange(slot_count, dtype=jnp.int32) * row_count + my_row
    current = choi
    for step in range(PANELS):
        row_tile = current[step // row_count]
        tile_row = broadcast(row_tile, "row", step % row_count)

        def build(operands):
            factor, inverse = factor_tile(operands[0])
            return panel_from(operands[1], factor, inverse, tile_index, step)

        def nothing(operands):
            return jnp.zeros_like(operands[1])

        panel_tiles = lax.cond(my_col == step, build, nothing, (tile_row, current))
        panel_tiles = broadcast(panel_tiles, "col", step)
        my_tile = lax.dynamic_index_in_dim(panel_tiles, my_col // row_count, 0, keepdims=False)
        partner = broadcast(my_tile, "row", my_col % row_count)
        updated = current - jnp.einsum(
            "sij,kj->sik", panel_tiles, partner, precision=lax.Precision.HIGHEST
        )
        trailing = (tile_index[:, None, None] > step) & (my_col > step)
        current = jnp.where(my_col == step, panel_tiles, jnp.where(trailing, updated, current))
    cleared = (my_col >= PANELS) & (tile_index[:, None, None] < PANELS)
    return jnp.where(cleared, 0.0, current)


def solution(mesh):
    return jax.shard_map(
        body,
        mesh=mesh,
        in_specs=(P(None, "row", "col"),),
        out_specs=P(None, "row", "col"),
        check_vma=False,
    )
```

profile of v0, /device:TPU:0, one launch (start us, length us, event | category | flops | bytes accessed | tf_op | source)
XLA Modules:
  0.0 474.8 jit_solution(8787741748421579258)
XLA Ops:
  6.5 1.7 select_bitcast_fusion.4
  8.3 58.7 %all-reduce.8.cloned.1.call-done = f32[256,256]{1,0:T(8,128)} async-done(((f32[256,256]{1,0:T(8,128)}), f32[256,256]{1,0:T(8,128)}) %all-reduce.8.cloned.1.call-update) | async-done | bytes 262160 | tf_op jit(solution)/shard_map/psum | solution.py:11
  67.0 63.7 %conditional.2 = (f32[4,256,256]{2,1,0:T(8,128)S(1)}) conditional(s32[]{:T(128)} %convert_element_type.21, () %tuple.20, (s32[4]{0:T(128)S(1)}, f32[256,256]{1,0:T(8,128)}, f32[4,256,256]{2,1,0:T(8,128)}) %tuple.21), branch_computations={%region_1.2_spmd, %region_2.9_spmd} | conditional | flops 1007927552 | bytes 15337775 | solution.py:46
  67.1 0.8 copy-done.2
  68.2 11.7 %cholesky.130 = f32[128,128]{1,0:T(8,128)S(1)} custom-call(f32[128,128]{1,0:T(8,128)S(1)} %cholesky.194), custom_call_target="Cholesky" | custom-call | tf_op jit(solution)/shard_map/cond/branch_1_fun/jit(cholesky)/cholesky | solution.py:17
  79.9 9.8 %custom-call.13 = f32[1,128,128]{1,2,0:T(8,128)S(1)} custom-call(f32[1,128,128]{2,1,0:T(8,128)S(1)} %get-tuple-element.82), custom_call_target="InvertDiagBlocksLowerTriangular" | custom-call | tf_op jit(solution)/shard_map/cond/branch_1_fun/jit(cholesky)/cholesky | solution.py:17
  90.0 0.3 convolution_subtract_fusion.1
  90.2 11.7 %cholesky.147 = f32[128,128]{1,0:T(8,128)S(1)} custom-call(f32[128,128]{1,0:T(8,128)S(1)} %convolution_subtract_fusion.1), custom_call_target="Cholesky" | custom-call | tf_op jit(solution)/shard_map/cond/branch_1_fun/jit(cholesky)/cholesky | solution.py:17
  102.0 0.7 compare_reduce_fusion
  104.2 4.3 while.4
  104.5 0.6 fusion.55
  105.0 1.4 bitcast_dynamic-update-slice_fusion.5
  106.5 0.6 fusion.55
  107.1 1.4 bitcast_dynamic-update-slice_fusion.5
  108.5 19.7 %custom-call.14 = f32[2,128,128]{1,2,0:T(8,128)S(1)} custom-call(f32[2,128,128]{2,1,0:T(8,128)S(1)} %get-tuple-element.45), custom_call_target="InvertDiagBlocksLowerTriangular" | custom-call | tf_op jit(solution)/shard_map/cond/branch_1_fun/jit(_solve_triangular)/triangular_solve | solution.py:18
  128.2 0.3 fusion.7
  128.8 0.3 fusion.10
  129.1 1.1 fusion
  130.2 0.3 copy.11
  130.8 1.1 broadcast_select_fusion.1
  131.9 48.6 %all-reduce.10.cloned.1.call-done = f32[4,256,256]{2,1,0:T(8,128)} async-done(((f32[4,256,256]{2,1,0:T(8,128)}), f32[4,256,256]{2,1,0:T(8,128)}) %all-reduce.10.cloned.1.call-update) | async-done | bytes 1048592 | tf_op jit(solution)/shard_map/psum | solution.py:11
  180.5 1.7 select_bitcast_fusion.3
  182.3 54.5 %all-reduce.12.cloned.1.call-done = f32[256,256]{1,0:T(8,128)} async-done(((f32[256,256]{1,0:T(8,128)}), f32[256,256]{1,0:T(8,128)}) %all-reduce.12.cloned.1.call-update) | async-done | bytes 262160 | tf_op jit(solution)/shard_map/psum | solution.py:11
  236.8 2.7 fusion.32
  239.5 0.7 fusion.33
  240.3 53.4 %all-reduce.14.cloned.1.call-done = f32[256,256]{1,0:T(8,128)} async-done(((f32[256,256]{1,0:T(8,128)}), f32[256,256]{1,0:T(8,128)}) %all-reduce.14.cloned.1.call-update) | async-done | bytes 262160 | tf_op jit(solution)/shard_map/psum | solution.py:11
  293.7 0.4 conditional.3
  294.1 1.1 broadcast_select_fusion
  295.2 113.0 %all-reduce.16.cloned.1.call-done = f32[4,256,256]{2,1,0:T(8,128)} async-done(((f32[4,256,256]{2,1,0:T(8,128)}), f32[4,256,256]{2,1,0:T(8,128)}) %all-reduce.16.cloned.1.call-update) | async-done | bytes 1048592 | tf_op jit(solution)/shard_map/psum | solution.py:11
  408.2 1.7 select_bitcast_fusion.2
  410.0 54.4 %all-reduce.18.cloned.1.call-done = f32[256,256]{1,0:T(8,128)} async-done(((f32[256,256]{1,0:T(8,128)}), f32[256,256]{1,0:T(8,128)}) %all-reduce.18.cloned.1.call-update) | async-done | bytes 262160 | tf_op jit(solution)/shard_map/psum | solution.py:11
  464.3 3.6 fusion.31
  (38 shorter events, 1.4 us)
Async XLA Ops:
  6.5 60.5 %all-reduce.8.cloned.1.call-start = ((), (), s32[]{:S(2)}) async-start(), calls=%async_computation | async-start | bytes 524288 | tf_op jit(solution)/shard_map/psum | solution.py:11
  8.2 172.3 %all-reduce.10.cloned.1.call-start = ((), (), s32[]{:S(2)}) async-start(), calls=%async_computation.1 | async-start | bytes 2097152 | tf_op jit(solution)/shard_map/psum | solution.py:11
  67.0 0.9 copy-start.2
  104.2 24.9 %copy-start.1 = (f32[4,256,256]{2,1,0:T(8,128)S(1)}, f32[4,256,256]{2,1,0:T(8,128)}, u32[]{:S(2)}) copy-start(f32[4,256,256]{2,1,0:T(8,128)} %get-tuple-element.26) | copy-start | bytes 3145732 | tf_op jit(solution)/shard_map/cond
  131.8 105.0 %copy-start = (f32[4,256,256]{2,1,0:T(8,128)S(1)}, f32[4,256,256]{2,1,0:T(8,128)}, u32[]{:S(2)}) copy-start(f32[4,256,256]{2,1,0:T(8,128)} %param.8) | copy-start | bytes 3145732
  131.9 104.9 %all-reduce.12.cloned.1.call-start = ((), (), s32[]{:S(2)}) async-start(), calls=%async_computation.2 | async-start | bytes 524288 | tf_op jit(solution)/shard_map/psum | solution.py:11
  182.2 111.4 %all-reduce.14.cloned.1.call-start = ((), (), s32[]{:S(2)}) async-start(), calls=%async_computation.3 | async-start | bytes 524288 | tf_op jit(solution)/shard_map/psum | solution.py:11
  240.2 168.0 %all-reduce.16.cloned.1.call-start = ((), (), s32[]{:S(2)}) async-start(), calls=%async_computation.4 | async-start | bytes 2097152 | tf_op jit(solution)/shard_map/psum | solution.py:11
  295.2 169.2 %all-reduce.18.cloned.1.call-start = ((), (), s32[]{:S(2)}) async-start(), calls=%async_computation.5 | async-start | bytes 524288 | tf_op jit(solution)/shard_map/psum | solution.py:11
Sparse Core Ops, SparseCore 0:
  10.4 56.5 all-reduce.7
  132.0 48.5 all-reduce.9
  183.6 53.1 all-reduce.11
  240.3 53.3 all-reduce.13
  295.9 112.3 all-reduce.15
  411.1 53.1 all-reduce.17
where the time goes:
time: 475 us
  waiting for transfers between devices  383 us (81%)
  other arithmetic  61.7 us (13%)
  between operations  13.6 us (3%)
  matrix products  8.71 us (2%)
  local copies, waits for them, and re-layouts  5.67 us (1%)
    psum x6, waiting for transfers between devices, broadcast(): return lax.psum(kept, axis)  383 us
    another operation x6, other arithmetic, factor_tile(): factor = jnp.linalg.cholesky(diagonal)  34 us
    another operation x4, other arithmetic, factor_tile(): inverse = jax.scipy.linalg.solve_triangular(factor, identity, lower=True)  19.7 us
  transfers between devices with their start and end apart: 6, of which 6 were waited for; matrix products, arithmetic and copies ran while one was open for 0% of the time, Pallas kernels for 0%

commit v1 on v0

--- a/solution.py
+++ b/solution.py
@@ -8,7 +8,7 @@
 
 def broadcast(value, axis, source):
     kept = jnp.where(lax.axis_index(axis) == source, value, 0).astype(value.dtype)
-    return lax.psum(kept, axis)
+    return jnp.sum(lax.all_gather(kept, axis), axis=0)
 
 
 def factor_tile(diagonal):

time: 475 us -> 430 us (0.905)
  waiting for transfers between devices: 383 us -> 333 us
  other arithmetic: 61.7 us -> 70.2 us
    psum x6 -> x0, waiting for transfers between devices: 383 us -> none  [broadcast(): return lax.psum(kept, axis)]
    all_gather x0 -> x6, waiting for transfers between devices: none -> 333 us  [broadcast(): return jnp.sum(lax.all_gather(kept, axis), axis=0)]
    reduce_sum x0 -> x5, other arithmetic: none -> 10.5 us  [broadcast(): return jnp.sum(lax.all_gather(kept, axis), axis=0)]
where the time goes in v1:
time: 430 us
  waiting for transfers between devices  333 us (77%)
  other arithmetic  70.2 us (16%)
  between operations  13.6 us (3%)
  matrix products  5.43 us (1%)
  local copies, waits for them, and re-layouts  4.67 us (1%)
    all_gather x6, waiting for transfers between devices, broadcast(): return jnp.sum(lax.all_gather(kept, axis), axis=0)  333 us
    another operation x6, other arithmetic, factor_tile(): factor = jnp.linalg.cholesky(diagonal)  34 us
    another operation x4, other arithmetic, factor_tile(): inverse = jax.scipy.linalg.solve_triangular(factor, identity, lower=True)  19.7 us
    reduce_sum x5, other arithmetic, broadcast(): return jnp.sum(lax.all_gather(kept, axis), axis=0)  10.5 us
  transfers between devices with their start and end apart: 6, of which 6 were waited for; matrix products, arithmetic and copies ran while one was open for 0% of the time, Pallas kernels for 0%

profile of v1, /device:TPU:0, one launch (start us, length us, event | category | flops | bytes accessed | tf_op | source)
XLA Modules:
  0.0 429.6 jit_solution(13317623542121607462)
XLA Ops:
  6.5 1.7 slice_select_fusion.1
  8.3 31.5 %all-gather.9.cloned.1.call-done = f32[8,256,256]{2,1,0:T(8,128)} async-done(((f32[1,256,256]{2,1,0:T(8,128)}), f32[8,256,256]{2,1,0:T(8,128)}) %all-gather.9.cloned.1.call-update) | async-done | bytes 2097168 | tf_op jit(solution)/shard_map/all_gather | solution.py:11
  39.8 64.3 %conditional.2 = (f32[4,256,256]{2,1,0:T(8,128)S(1)}) conditional(s32[]{:T(128)} %convert_element_type.21, () %tuple.20, (s32[4]{0:T(128)S(1)}, f32[8,256,256]{2,1,0:T(8,128)}, f32[4,256,256]{2,1,0:T(8,128)}) %tuple.21), branch_computations={%region_0.1_spmd, %region_1.9_spmd} | conditional | flops 1008386304 | bytes 16648471 | solution.py:46
  39.8 1.8 reduce_sum.50
  41.8 11.7 %cholesky.130 = f32[128,128]{1,0:T(8,128)S(1)} custom-call(f32[128,128]{1,0:T(8,128)S(1)} %cholesky.194), custom_call_target="Cholesky" | custom-call | tf_op jit(solution)/shard_map/cond/branch_1_fun/jit(cholesky)/cholesky | solution.py:17
  53.6 9.8 %custom-call.13 = f32[1,128,128]{1,2,0:T(8,128)S(1)} custom-call(f32[1,128,128]{2,1,0:T(8,128)S(1)} %get-tuple-element.80), custom_call_target="InvertDiagBlocksLowerTriangular" | custom-call | tf_op jit(solution)/shard_map/cond/branch_1_fun/jit(cholesky)/cholesky | solution.py:17
  63.9 11.7 %cholesky.147 = f32[128,128]{1,0:T(8,128)S(1)} custom-call(f32[128,128]{1,0:T(8,128)S(1)} %convolution_subtract_fusion.1), custom_call_target="Cholesky" | custom-call | tf_op jit(solution)/shard_map/cond/branch_1_fun/jit(cholesky)/cholesky | solution.py:17
  75.7 0.7 compare_reduce_fusion
  77.8 4.1 while.4
  78.0 0.6 fusion.54
  78.5 1.4 bitcast_dynamic-update-slice_fusion.5
  79.9 0.6 fusion.54
  80.5 1.4 bitcast_dynamic-update-slice_fusion.5
  81.9 19.7 %custom-call.14 = f32[2,128,128]{1,2,0:T(8,128)S(1)} custom-call(f32[2,128,128]{2,1,0:T(8,128)S(1)} %get-tuple-element.49), custom_call_target="InvertDiagBlocksLowerTriangular" | custom-call | tf_op jit(solution)/shard_map/cond/branch_1_fun/jit(_solve_triangular)/triangular_solve | solution.py:18
  102.5 1.1 fusion
  104.1 1.1 broadcast_select_fusion.1
  105.3 78.1 %all-gather.17.cloned.1.call-done = f32[16,256,256]{2,1,0:T(8,128)} async-done(((f32[4,256,256]{2,1,0:T(8,128)}), f32[16,256,256]{2,1,0:T(8,128)}) %all-gather.17.cloned.1.call-update) | async-done | bytes 4194320 | tf_op jit(solution)/shard_map/all_gather | solution.py:11
  183.3 2.6 reduce_sum.56
  185.9 0.7 dynamic-slice_select_fusion.1
  186.8 26.3 %all-gather.11.cloned.1.call-done = f32[8,256,256]{2,1,0:T(8,128)} async-done(((f32[1,256,256]{2,1,0:T(8,128)}), f32[8,256,256]{2,1,0:T(8,128)}) %all-gather.11.cloned.1.call-update) | async-done | bytes 2097168 | tf_op jit(solution)/shard_map/all_gather | solution.py:11
  213.1 1.8 reduce_sum.57
  214.9 1.0 fusion.32
  215.9 0.7 slice_select_fusion
  216.7 27.9 %all-gather.13.cloned.1.call-done = f32[8,256,256]{2,1,0:T(8,128)} async-done(((f32[1,256,256]{2,1,0:T(8,128)}), f32[8,256,256]{2,1,0:T(8,128)}) %all-gather.13.cloned.1.call-update) | async-done | bytes 2097168 | tf_op jit(solution)/shard_map/all_gather | solution.py:11
  244.6 0.4 conditional.3
  245.0 1.1 broadcast_select_fusion
  246.1 143.1 %all-gather.19.cloned.1.call-done = f32[16,256,256]{2,1,0:T(8,128)} async-done(((f32[4,256,256]{2,1,0:T(8,128)}), f32[16,256,256]{2,1,0:T(8,128)}) %all-gather.19.cloned.1.call-update) | async-done | bytes 4194320 | tf_op jit(solution)/shard_map/all_gather | solution.py:11
  389.2 2.6 reduce_sum.58
  391.8 0.7 dynamic-slice_select_fusion
  392.6 26.4 %all-gather.15.cloned.1.call-done = f32[8,256,256]{2,1,0:T(8,128)} async-done(((f32[1,256,256]{2,1,0:T(8,128)}), f32[8,256,256]{2,1,0:T(8,128)}) %all-gather.15.cloned.1.call-update) | async-done | bytes 2097168 | tf_op jit(solution)/shard_map/all_gather | solution.py:11
  419.0 1.8 reduce_sum.59
  420.8 2.0 fusion.31
  (41 shorter events, 2.6 us)
Async XLA Ops:
  6.5 33.2 %all-gather.9.cloned.1.call-start = ((), (), s32[]{:S(2)}) async-start(), calls=%async_computation | async-start | bytes 2359296 | tf_op jit(solution)/shard_map/all_gather | solution.py:11
  8.2 175.1 %all-gather.17.cloned.1.call-start = ((), (), s32[]{:S(2)}) async-start(), calls=%async_computation.4 | async-start | bytes 5242880 | tf_op jit(solution)/shard_map/all_gather | solution.py:11
  63.4 39.1 %copy-start.1 = (f32[4,256,256]{2,1,0:T(8,128)S(1)}, f32[4,256,256]{2,1,0:T(8,128)}, u32[]{:S(2)}) copy-start(f32[4,256,256]{2,1,0:T(8,128)} %get-tuple-element.31) | copy-start | bytes 3145732 | tf_op jit(solution)/shard_map/cond
  105.2 107.9 %all-gather.11.cloned.1.call-start = ((), (), s32[]{:S(2)}) async-start(), calls=%async_computation.1 | async-start | bytes 2359296 | tf_op jit(solution)/shard_map/all_gather | solution.py:11
  185.9 28.9 %copy-start = (f32[4,256,256]{2,1,0:T(8,128)S(1)}, f32[4,256,256]{2,1,0:T(8,128)}, u32[]{:S(2)}) copy-start(f32[4,256,256]{2,1,0:T(8,128)} %param.8) | copy-start | bytes 3145732
  186.7 57.9 %all-gather.13.cloned.1.call-start = ((), (), s32[]{:S(2)}) async-start(), calls=%async_computation.2 | async-start | bytes 2359296 | tf_op jit(solution)/shard_map/all_gather | solution.py:11
  216.7 172.6 %all-gather.19.cloned.1.call-start = ((), (), s32[]{:S(2)}) async-start(), calls=%async_computation.5 | async-start | bytes 5242880 | tf_op jit(solution)/shard_map/all_gather | solution.py:11
  246.1 172.9 %all-gather.15.cloned.1.call-start = ((), (), s32[]{:S(2)}) async-start(), calls=%async_computation.3 | async-start | bytes 2359296 | tf_op jit(solution)/shard_map/all_gather | solution.py:11
Sparse Core Ops, SparseCore 0:
  9.2 30.4 all-gather.8
  105.3 77.9 all-gather.16
  186.8 26.2 all-gather.10
  216.8 27.7 all-gather.12
  246.2 142.9 all-gather.18
  392.7 26.2 all-gather.14
